TPU v7x, 128 devices: a whole 4x4x4 slice. The times are simulated.
128 devices in a mesh: bx: 8 (over y, x_hi), by: 16 (over x_lo, z, core).
Axes of the slice: x: 4 (x_hi: 2, x_lo: 2; x = x_hi * 2 + x_lo), y: 4, z: 4, core: 2. Of those that a mesh axis runs over, the one named last changes fastest.
Arguments:
- speed_vectors: float32 [3, 6, 120, 240, 128], P(None, None, 'bx', 'by'), may hold values from -10 to 10, as said below
- bin_population: int32 [120, 240, 128], P('bx', 'by'), may hold values from 0 to 6, as said below
- spin_choice: int32 [12, 120, 240, 128], P(None, 'bx', 'by'), may hold values from 0 to 5
- approval_flags: int32 [12, 120, 240, 128], P(None, 'bx', 'by'), may hold values 0 or 1
- round_evenness: int32 [12], replicated, may hold values from 0 to 1
- grid_displacements: int32 [12], replicated, may hold values from 0 to 127
- thermostat_heat_level: float32 [12], replicated, may hold values from 0.5 to 2
Outputs:
- final_velocity: float32 [3, 6, 120, 240, 128], P(None, None, 'bx', 'by')
Inputs may be any that keep to these rules, and one draw needn't show every extreme that they name: `bin_population`: A cell's particles fill its first slots. `speed_vectors`: entries in slots at or beyond a cell's occupancy are not read.
All inputs are finite; a program needn't handle non-finite values. No bound on the sum of `approval_flags` on one device may be relied on, other than what follows from the above.
Results may differ from a plain program's by a relative error of at most 0.0003.
Values sent between devices are 32-bit elements; how exact they have to be, the bound alone decides.
No kernel may reach another device: no remote copies, remote signals or barrier semaphores. Data moves between devices by JAX's collectives and lax.ppermute only.
A program may use at most 64 MiB of HBM per device.

v0:
```python
import math
import jax
import jax.numpy as jnp
from jax import lax
from jax.sharding import Mesh
from jax.sharding import PartitionSpec as P

ROUNDS = 6
BX_BY = ("bx_0", "bx_1", "by_0", "by_1", "by_2")
BX = ("bx_0", "bx_1")
BY = ("by_0", "by_1", "by_2")
turn_angle = 130.0 * math.pi / 180.0
drag_gain = 1.0
excess_coupling = 1e-06


def over_axes(array, axes):
    for axis in axes:
        array = lax.psum(array, axis)
    return array


def from_behind(value, axis, steps):
    count = lax.axis_size(axis)
    pairs = [(source, (source + steps) % count) for source in range(count)]
    return lax.ppermute(value, axis, pairs)


def rotate(thermal, spin_choice):
    picked = spin_choice // 2
    unit_axis = [(picked == member).astype(jnp.float32)[None] for member in range(3)]
    sine_term = (math.sin(turn_angle) * (1 - 2 * (spin_choice % 2)).astype(jnp.float32))[None]
    cosine_term = math.cos(turn_angle)
    along_axis = unit_axis[0] * thermal[0] + unit_axis[1] * thermal[1] + unit_axis[2] * thermal[2]
    result = []
    for member in range(3):
        second = (member + 1) % 3
        third_idx = (member + 2) % 3
        cross_term = unit_axis[second] * thermal[third_idx] - unit_axis[third_idx] * thermal[second]
        result.append(
            cosine_term * thermal[member]
            + (1.0 - cosine_term) * unit_axis[member] * along_axis
            + sine_term * cross_term
        )
    return jnp.stack(result)


def per_device(
    speed_vectors,
    bin_population,
    spin_choice,
    approval_flags,
    round_evenness,
    grid_displacements,
    thermostat_heat_level,
):
    slot_count = speed_vectors.shape[1]
    overall_work_sum = over_axes(jnp.sum(bin_population.astype(jnp.float32)), BX_BY)

    def decode(received):
        return (received[1], received[0], received[2])

    def collide_step(
        ensemble_snapshot, bin_tallies, pending, present_round_number, partner_heading
    ):
        slot_rank = lax.broadcasted_iota(jnp.int32, (slot_count,) + bin_tallies.shape, 0)
        occupied = (slot_rank < bin_tallies[None]).astype(jnp.float32)
        moment = jnp.sum(ensemble_snapshot * occupied[None], axis=1)
        cell_mass = bin_tallies.astype(jnp.float32)
        safe_mass = jnp.maximum(cell_mass, 1.0)
        accept_bits = approval_flags[present_round_number].astype(jnp.float32)
        along_moment = moment[partner_heading]
        step_parity = round_evenness[present_round_number]
        stack_parts = (along_moment[None], cell_mass[None], accept_bits[None])
        extent = bin_tallies.shape[partner_heading]
        low_edge = jnp.concatenate(
            [
                lax.slice_in_dim(part_item, 0, 1, axis=partner_heading + 1)
                for part_item in stack_parts
            ],
            0,
        )
        high_edge = jnp.concatenate(
            [
                lax.slice_in_dim(part_item, extent - 1, extent, axis=partner_heading + 1)
                for part_item in stack_parts
            ],
            0,
        )
        if partner_heading == 0:
            start = lax.axis_index(BX) * extent
        else:
            start = lax.axis_index(BY) * extent
        if partner_heading == 0:
            from_above = from_behind(low_edge, BX, -1)
            from_below = from_behind(high_edge, BX, 1)
        else:
            from_above = from_behind(low_edge, BY, -1)
            from_below = from_behind(high_edge, BY, 1)
        above_parts = decode(from_above)
        below_parts = decode(from_below)
        coords = start + lax.broadcasted_iota(jnp.int32, bin_tallies.shape, partner_heading)
        is_lower = (coords - step_parity) % 2 == 0

        def partner(local_values, below_values, above_values):
            extended = jnp.concatenate([below_values, local_values, above_values], partner_heading)
            upper_side = lax.slice_in_dim(extended, 2, extent + 2, axis=partner_heading)
            lower_side = lax.slice_in_dim(extended, 0, extent, axis=partner_heading)
            return jnp.where(is_lower, upper_side, lower_side)

        other_mass = partner(cell_mass, below_parts[0], above_parts[0])
        other_moment = partner(along_moment, below_parts[1], above_parts[1])
        other_bits = partner(accept_bits, below_parts[2], above_parts[2])
        own_speed = pending * along_moment / safe_mass
        other_speed = pending * other_moment / jnp.maximum(other_mass, 1.0)
        closing = jnp.maximum(
            jnp.where(is_lower, own_speed - other_speed, other_speed - own_speed), 0.0
        )
        reduced = cell_mass * other_mass / jnp.maximum(cell_mass + other_mass, 1.0)
        transfer = (
            jnp.maximum(accept_bits, other_bits) * reduced * closing * jnp.tanh(drag_gain * closing)
        )
        new_along = pending * along_moment - jnp.where(is_lower, transfer, -transfer)
        true_moment = jnp.stack(
            [
                new_along if member == partner_heading else pending * moment[member]
                for member in range(3)
            ]
        )
        thermal = (ensemble_snapshot - (moment / safe_mass)[:, None]) * occupied[None]
        kinetic_local = jnp.sum(
            true_moment * true_moment / safe_mass
        ) + pending * pending * jnp.sum(thermal * thermal)
        motion_work_sum = over_axes(kinetic_local, BX_BY)
        speed_multiplier = jnp.sqrt(
            3.0
            * thermostat_heat_level[present_round_number]
            * overall_work_sum
            / (motion_work_sum + excess_coupling)
        )
        turned = rotate(thermal, spin_choice[present_round_number])
        return (
            speed_multiplier
            * ((true_moment / safe_mass)[:, None] * occupied[None] + pending * turned),
            pending,
        )

    def one_round(round_index, carry):
        ensemble_snapshot, bin_tallies, pending = carry
        for displacement_amount in range(2):
            present_round_number = 2 * round_index + displacement_amount
            ensemble_snapshot, pending = collide_step(
                ensemble_snapshot, bin_tallies, pending, present_round_number, displacement_amount
            )
            shift_by = grid_displacements[present_round_number]
            ensemble_snapshot = jnp.roll(ensemble_snapshot, shift_by, axis=4)
            bin_tallies = jnp.roll(bin_tallies, shift_by, axis=2)
        return (ensemble_snapshot, bin_tallies, pending)

    start_scale = jnp.ones((), jnp.float32)
    ensemble_snapshot, bin_tallies, pending = lax.fori_loop(
        0, ROUNDS, one_round, (speed_vectors, bin_population, start_scale)
    )
    return ensemble_snapshot


def solution(mesh):
    split = Mesh(mesh.devices.reshape(4, 2, 2, 4, 2), ("bx_0", "bx_1", "by_0", "by_1", "by_2"))
    return jax.shard_map(
        per_device,
        mesh=split,
        in_specs=(
            P(None, None, BX, BY, None),
            P(BX, BY, None),
            P(None, BX, BY, None),
            P(None, BX, BY, None),
            P(),
            P(),
            P(),
        ),
        out_specs=P(None, None, BX, BY, None),
        check_vma=False,
    )
```

profile of v0, /device:TPU:47, one launch (start us, length us, event | category | flops | bytes accessed | tf_op | source)
XLA Modules:
  0.0 786.4 jit_solution(3658337964983819190)
XLA Ops:
  4.7 7.3 psum.185
  22.4 7.7 psum.188
  30.0 9.8 %psum.189 = f32[]{:T(128)} all-reduce(f32[]{:T(128)} %psum.188), channel_id=1, replica_groups=mesh['bx_0'=4,'bx_1'=2,'by_0'=2,'by_1'=4,'by_2'=2] {'by_2'}, use_global_device_ids=true, to_apply=%region_5.0 | all-reduce | flops 1 | bytes 8 | tf_op jit(solution)/shard_map/psum | solution.py:19
  39.8 746.6 %while.18 = (s32[]{:T(128)}, f32[3,6,15,15,128]{4,3,2,1,0:T(8,128)}, s32[15,15,128]{2,1,0:T(8,128)S(1)}, f32[12]{0:T(128)}, f32[]{:T(128)}, /*index=5*/s32[12]{0...) while((s32[]{:T(128)}, ...), condition=%wide.region_23.26_spmd, body=%wide.region_6.25_spmd.sunk | while | flops 29883296 | bytes 69046136 | solution.py:161
  70.2 8.8 %psum.200 = f32[]{:T(128)} all-reduce(f32[]{:T(128)S(6)} %add.745), channel_id=1, replica_groups=mesh['bx_0'=4,'bx_1'=2,'by_0'=2,'by_1'=4,'by_2'=2] {'bx_0'}, use_global_device_ids=true, to_apply=%region_10.10 | all-reduce | flops 1 | bytes 8 | tf_op jit(solution)/shard_map/while/body/eval_jaxpr/psum | solution.py:19
  79.0 6.0 psum.201
  90.6 9.1 %psum.203 = f32[]{:T(128)} all-reduce(f32[]{:T(128)} %psum.202), channel_id=1, replica_groups=mesh['bx_0'=4,'bx_1'=2,'by_0'=2,'by_1'=4,'by_2'=2] {'by_1'}, use_global_device_ids=true, to_apply=%region_13.13 | all-reduce | flops 1 | bytes 8 | tf_op jit(solution)/shard_map/while/body/eval_jaxpr/psum | solution.py:19
  100.4 9.9 %psum.204 = f32[]{:T(128)} all-reduce(f32[]{:T(128)} %psum.203), channel_id=1, replica_groups=mesh['bx_0'=4,'bx_1'=2,'by_0'=2,'by_1'=4,'by_2'=2] {'by_2'}, use_global_device_ids=true, to_apply=%region_14.14 | all-reduce | flops 1 | bytes 8 | tf_op jit(solution)/shard_map/while/body/eval_jaxpr/psum | solution.py:19
  122.5 7.2 psum.205
  129.7 5.9 psum.206
  141.2 7.4 psum.208
  148.6 12.5 %psum.209 = f32[]{:T(128)} all-reduce(f32[]{:T(128)} %psum.208), channel_id=1, replica_groups=mesh['bx_0'=4,'bx_1'=2,'by_0'=2,'by_1'=4,'by_2'=2] {'by_2'}, use_global_device_ids=true, to_apply=%region_22.24 | all-reduce | flops 1 | bytes 8 | tf_op jit(solution)/shard_map/while/body/eval_jaxpr/psum | solution.py:19
  196.9 7.3 psum.200
  204.3 6.0 psum.201
  216.0 6.3 psum.203
  222.9 9.9 %psum.204 = f32[]{:T(128)} all-reduce(f32[]{:T(128)} %psum.203), channel_id=1, replica_groups=mesh['bx_0'=4,'bx_1'=2,'by_0'=2,'by_1'=4,'by_2'=2] {'by_2'}, use_global_device_ids=true, to_apply=%region_14.14 | all-reduce | flops 1 | bytes 8 | tf_op jit(solution)/shard_map/while/body/eval_jaxpr/psum | solution.py:19
  245.0 8.4 %psum.205 = f32[]{:T(128)} all-reduce(f32[]{:T(128)S(6)} %add.749), channel_id=1, replica_groups=mesh['bx_0'=4,'bx_1'=2,'by_0'=2,'by_1'=4,'by_2'=2] {'bx_0'}, use_global_device_ids=true, to_apply=%region_18.20 | all-reduce | flops 1 | bytes 8 | tf_op jit(solution)/shard_map/while/body/eval_jaxpr/psum | solution.py:19
  253.4 5.9 psum.206
  264.9 8.5 %psum.208 = f32[]{:T(128)} all-reduce(f32[]{:T(128)} %psum.207), channel_id=1, replica_groups=mesh['bx_0'=4,'bx_1'=2,'by_0'=2,'by_1'=4,'by_2'=2] {'by_1'}, use_global_device_ids=true, to_apply=%region_21.23 | all-reduce | flops 1 | bytes 8 | tf_op jit(solution)/shard_map/while/body/eval_jaxpr/psum | solution.py:19
  273.4 11.7 %psum.209 = f32[]{:T(128)} all-reduce(f32[]{:T(128)} %psum.208), channel_id=1, replica_groups=mesh['bx_0'=4,'bx_1'=2,'by_0'=2,'by_1'=4,'by_2'=2] {'by_2'}, use_global_device_ids=true, to_apply=%region_22.24 | all-reduce | flops 1 | bytes 8 | tf_op jit(solution)/shard_map/while/body/eval_jaxpr/psum | solution.py:19
  321.1 6.6 psum.200
  327.7 6.0 psum.201
  339.4 6.3 psum.203
  346.3 9.6 %psum.204 = f32[]{:T(128)} all-reduce(f32[]{:T(128)} %psum.203), channel_id=1, replica_groups=mesh['bx_0'=4,'bx_1'=2,'by_0'=2,'by_1'=4,'by_2'=2] {'by_2'}, use_global_device_ids=true, to_apply=%region_14.14 | all-reduce | flops 1 | bytes 8 | tf_op jit(solution)/shard_map/while/body/eval_jaxpr/psum | solution.py:19
  368.0 9.4 %psum.205 = f32[]{:T(128)} all-reduce(f32[]{:T(128)S(6)} %add.749), channel_id=1, replica_groups=mesh['bx_0'=4,'bx_1'=2,'by_0'=2,'by_1'=4,'by_2'=2] {'bx_0'}, use_global_device_ids=true, to_apply=%region_18.20 | all-reduce | flops 1 | bytes 8 | tf_op jit(solution)/shard_map/while/body/eval_jaxpr/psum | solution.py:19
  389.0 8.5 %psum.208 = f32[]{:T(128)} all-reduce(f32[]{:T(128)} %psum.207), channel_id=1, replica_groups=mesh['bx_0'=4,'bx_1'=2,'by_0'=2,'by_1'=4,'by_2'=2] {'by_1'}, use_global_device_ids=true, to_apply=%region_21.23 | all-reduce | flops 1 | bytes 8 | tf_op jit(solution)/shard_map/while/body/eval_jaxpr/psum | solution.py:19
  397.5 11.3 %psum.209 = f32[]{:T(128)} all-reduce(f32[]{:T(128)} %psum.208), channel_id=1, replica_groups=mesh['bx_0'=4,'bx_1'=2,'by_0'=2,'by_1'=4,'by_2'=2] {'by_2'}, use_global_device_ids=true, to_apply=%region_22.24 | all-reduce | flops 1 | bytes 8 | tf_op jit(solution)/shard_map/while/body/eval_jaxpr/psum | solution.py:19
  444.8 6.6 psum.200
  451.4 6.0 psum.201
  463.1 6.3 psum.203
  470.0 9.6 %psum.204 = f32[]{:T(128)} all-reduce(f32[]{:T(128)} %psum.203), channel_id=1, replica_groups=mesh['bx_0'=4,'bx_1'=2,'by_0'=2,'by_1'=4,'by_2'=2] {'by_2'}, use_global_device_ids=true, to_apply=%region_14.14 | all-reduce | flops 1 | bytes 8 | tf_op jit(solution)/shard_map/while/body/eval_jaxpr/psum | solution.py:19
  491.8 9.4 %psum.205 = f32[]{:T(128)} all-reduce(f32[]{:T(128)S(6)} %add.749), channel_id=1, replica_groups=mesh['bx_0'=4,'bx_1'=2,'by_0'=2,'by_1'=4,'by_2'=2] {'bx_0'}, use_global_device_ids=true, to_apply=%region_18.20 | all-reduce | flops 1 | bytes 8 | tf_op jit(solution)/shard_map/while/body/eval_jaxpr/psum | solution.py:19
  512.8 8.5 %psum.208 = f32[]{:T(128)} all-reduce(f32[]{:T(128)} %psum.207), channel_id=1, replica_groups=mesh['bx_0'=4,'bx_1'=2,'by_0'=2,'by_1'=4,'by_2'=2] {'by_1'}, use_global_device_ids=true, to_apply=%region_21.23 | all-reduce | flops 1 | bytes 8 | tf_op jit(solution)/shard_map/while/body/eval_jaxpr/psum | solution.py:19
  521.3 11.7 %psum.209 = f32[]{:T(128)} all-reduce(f32[]{:T(128)} %psum.208), channel_id=1, replica_groups=mesh['bx_0'=4,'bx_1'=2,'by_0'=2,'by_1'=4,'by_2'=2] {'by_2'}, use_global_device_ids=true, to_apply=%region_22.24 | all-reduce | flops 1 | bytes 8 | tf_op jit(solution)/shard_map/while/body/eval_jaxpr/psum | solution.py:19
  568.9 6.6 psum.200
  575.5 6.0 psum.201
  587.2 6.3 psum.203
  594.1 9.6 %psum.204 = f32[]{:T(128)} all-reduce(f32[]{:T(128)} %psum.203), channel_id=1, replica_groups=mesh['bx_0'=4,'bx_1'=2,'by_0'=2,'by_1'=4,'by_2'=2] {'by_2'}, use_global_device_ids=true, to_apply=%region_14.14 | all-reduce | flops 1 | bytes 8 | tf_op jit(solution)/shard_map/while/body/eval_jaxpr/psum | solution.py:19
  615.9 9.4 %psum.205 = f32[]{:T(128)} all-reduce(f32[]{:T(128)S(6)} %add.749), channel_id=1, replica_groups=mesh['bx_0'=4,'bx_1'=2,'by_0'=2,'by_1'=4,'by_2'=2] {'bx_0'}, use_global_device_ids=true, to_apply=%region_18.20 | all-reduce | flops 1 | bytes 8 | tf_op jit(solution)/shard_map/while/body/eval_jaxpr/psum | solution.py:19
  636.9 8.5 %psum.208 = f32[]{:T(128)} all-reduce(f32[]{:T(128)} %psum.207), channel_id=1, replica_groups=mesh['bx_0'=4,'bx_1'=2,'by_0'=2,'by_1'=4,'by_2'=2] {'by_1'}, use_global_device_ids=true, to_apply=%region_21.23 | all-reduce | flops 1 | bytes 8 | tf_op jit(solution)/shard_map/while/body/eval_jaxpr/psum | solution.py:19
  645.4 11.3 %psum.209 = f32[]{:T(128)} all-reduce(f32[]{:T(128)} %psum.208), channel_id=1, replica_groups=mesh['bx_0'=4,'bx_1'=2,'by_0'=2,'by_1'=4,'by_2'=2] {'by_2'}, use_global_device_ids=true, to_apply=%region_22.24 | all-reduce | flops 1 | bytes 8 | tf_op jit(solution)/shard_map/while/body/eval_jaxpr/psum | solution.py:19
  692.6 6.6 psum.200
  699.3 6.0 psum.201
  710.9 6.3 psum.203
  717.9 9.6 %psum.204 = f32[]{:T(128)} all-reduce(f32[]{:T(128)} %psum.203), channel_id=1, replica_groups=mesh['bx_0'=4,'bx_1'=2,'by_0'=2,'by_1'=4,'by_2'=2] {'by_2'}, use_global_device_ids=true, to_apply=%region_14.14 | all-reduce | flops 1 | bytes 8 | tf_op jit(solution)/shard_map/while/body/eval_jaxpr/psum | solution.py:19
  739.6 9.4 %psum.205 = f32[]{:T(128)} all-reduce(f32[]{:T(128)S(6)} %add.749), channel_id=1, replica_groups=mesh['bx_0'=4,'bx_1'=2,'by_0'=2,'by_1'=4,'by_2'=2] {'bx_0'}, use_global_device_ids=true, to_apply=%region_18.20 | all-reduce | flops 1 | bytes 8 | tf_op jit(solution)/shard_map/while/body/eval_jaxpr/psum | solution.py:19
  760.6 8.5 %psum.208 = f32[]{:T(128)} all-reduce(f32[]{:T(128)} %psum.207), channel_id=1, replica_groups=mesh['bx_0'=4,'bx_1'=2,'by_0'=2,'by_1'=4,'by_2'=2] {'by_1'}, use_global_device_ids=true, to_apply=%region_21.23 | all-reduce | flops 1 | bytes 8 | tf_op jit(solution)/shard_map/while/body/eval_jaxpr/psum | solution.py:19
  769.1 11.7 %psum.209 = f32[]{:T(128)} all-reduce(f32[]{:T(128)} %psum.208), channel_id=1, replica_groups=mesh['bx_0'=4,'bx_1'=2,'by_0'=2,'by_1'=4,'by_2'=2] {'by_2'}, use_global_device_ids=true, to_apply=%region_22.24 | all-reduce | flops 1 | bytes 8 | tf_op jit(solution)/shard_map/while/body/eval_jaxpr/psum | solution.py:19
  (481 shorter events, 334.0 us)
Async XLA Ops:
  0.9 38.9 %copy-start.8 = (s32[12]{0:T(128)S(1)}, s32[12]{0:T(128)}, u32[]{:S(2)}) copy-start(s32[12]{0:T(128)} %param.17) | copy-start | bytes 148
  0.9 38.9 %copy-start.10 = (s32[12]{0:T(128)S(1)}, s32[12]{0:T(128)}, u32[]{:S(2)}) copy-start(s32[12]{0:T(128)} %param.18) | copy-start | bytes 148
  46.4 14.8 %collective-permute-start.1 = (f32[3,1,15,128]{3,2,1,0:T(8,128)}, f32[3,1,15,128]{3,2,1,0:T(8,128)}, u32[]{:S(2)}, u32[]{:S(2)}) collective-permute-start(f32[3,1,15,128]{3,2,1,0:T(8,128)} %pad_maximum_fusion.23), channel_id=1, source_target_pairs={{0,112},{16,0},{32,16},{48,32},{64,48},{80,64},{96,80},{112,96},{1... | collective-permute-start | bytes 69128 | tf_op jit(solution)/shard_map/while/body/eval_jaxpr/ppermute | solution.py:26
  48.1 14.0 %collective-permute-start = (f32[3,1,15,128]{3,2,1,0:T(8,128)}, f32[3,1,15,128]{3,2,1,0:T(8,128)}, u32[]{:S(2)}, u32[]{:S(2)}) collective-permute-start(f32[3,1,15,128]{3,2,1,0:T(8,128)} %pad_maximum_fusion.22), channel_id=1, source_target_pairs={{0,16},{16,32},{32,48},{48,64},{64,80},{80,96},{96,112},{112,0},{1... | collective-permute-start | bytes 69128 | tf_op jit(solution)/shard_map/while/body/eval_jaxpr/ppermute | solution.py:26
  65.7 19.2 %copy-start.7 = (f32[12]{0:T(128)S(1)}, f32[12]{0:T(128)}, u32[]{:S(2)}) copy-start(f32[12]{0:T(128)} %get-tuple-element.660) | copy-start | bytes 148 | tf_op jit(solution)/shard_map/while
  65.7 45.4 %copy-start.1 = (f32[15,15,128]{2,1,0:T(8,128)S(1)}, f32[15,15,128]{2,1,0:T(8,128)}, u32[]{:S(2)}) copy-start(f32[15,15,128]{2,1,0:T(8,128)} %get-tuple-element.553) | copy-start | bytes 345604 | tf_op jit(solution)/shard_map/while
  65.7 45.4 %copy-start.2 = (f32[15,15,128]{2,1,0:T(8,128)S(1)}, f32[15,15,128]{2,1,0:T(8,128)}, u32[]{:S(2)}) copy-start(f32[15,15,128]{2,1,0:T(8,128)} %get-tuple-element.561) | copy-start | bytes 345604 | tf_op jit(solution)/shard_map/while
  65.7 45.4 %copy-start.3 = (f32[15,15,128]{2,1,0:T(8,128)S(1)}, f32[15,15,128]{2,1,0:T(8,128)}, u32[]{:S(2)}) copy-start(f32[15,15,128]{2,1,0:T(8,128)} %get-tuple-element.556) | copy-start | bytes 345604 | tf_op jit(solution)/shard_map/while
  115.1 3.4 collective-permute-start.3
  115.5 2.9 collective-permute-start.2
  173.1 14.8 %collective-permute-start.1 = (f32[3,1,15,128]{3,2,1,0:T(8,128)}, f32[3,1,15,128]{3,2,1,0:T(8,128)}, u32[]{:S(2)}, u32[]{:S(2)}) collective-permute-start(f32[3,1,15,128]{3,2,1,0:T(8,128)} %pad_maximum_fusion.23), channel_id=1, source_target_pairs={{0,112},{16,0},{32,16},{48,32},{64,48},{80,64},{96,80},{112,96},{1... | collective-permute-start | bytes 69128 | tf_op jit(solution)/shard_map/while/body/eval_jaxpr/ppermute | solution.py:26
  174.1 14.8 %collective-permute-start = (f32[3,1,15,128]{3,2,1,0:T(8,128)}, f32[3,1,15,128]{3,2,1,0:T(8,128)}, u32[]{:S(2)}, u32[]{:S(2)}) collective-permute-start(f32[3,1,15,128]{3,2,1,0:T(8,128)} %pad_maximum_fusion.22), channel_id=1, source_target_pairs={{0,16},{16,32},{32,48},{48,64},{64,80},{80,96},{96,112},{112,0},{1... | collective-permute-start | bytes 69128 | tf_op jit(solution)/shard_map/while/body/eval_jaxpr/ppermute | solution.py:26
  192.5 17.8 %copy-start.7 = (f32[12]{0:T(128)S(1)}, f32[12]{0:T(128)}, u32[]{:S(2)}) copy-start(f32[12]{0:T(128)} %get-tuple-element.660) | copy-start | bytes 148 | tf_op jit(solution)/shard_map/while
  192.5 41.2 %copy-start.1 = (f32[15,15,128]{2,1,0:T(8,128)S(1)}, f32[15,15,128]{2,1,0:T(8,128)}, u32[]{:S(2)}) copy-start(f32[15,15,128]{2,1,0:T(8,128)} %get-tuple-element.553) | copy-start | bytes 345604 | tf_op jit(solution)/shard_map/while
  192.5 41.2 %copy-start.2 = (f32[15,15,128]{2,1,0:T(8,128)S(1)}, f32[15,15,128]{2,1,0:T(8,128)}, u32[]{:S(2)}) copy-start(f32[15,15,128]{2,1,0:T(8,128)} %get-tuple-element.561) | copy-start | bytes 345604 | tf_op jit(solution)/shard_map/while
  192.5 41.2 %copy-start.3 = (f32[15,15,128]{2,1,0:T(8,128)S(1)}, f32[15,15,128]{2,1,0:T(8,128)}, u32[]{:S(2)}) copy-start(f32[15,15,128]{2,1,0:T(8,128)} %get-tuple-element.556) | copy-start | bytes 345604 | tf_op jit(solution)/shard_map/while
  237.6 3.3 collective-permute-start.3
  238.0 2.9 collective-permute-start.2
  297.3 14.8 %collective-permute-start.1 = (f32[3,1,15,128]{3,2,1,0:T(8,128)}, f32[3,1,15,128]{3,2,1,0:T(8,128)}, u32[]{:S(2)}, u32[]{:S(2)}) collective-permute-start(f32[3,1,15,128]{3,2,1,0:T(8,128)} %pad_maximum_fusion.23), channel_id=1, source_target_pairs={{0,112},{16,0},{32,16},{48,32},{64,48},{80,64},{96,80},{112,96},{1... | collective-permute-start | bytes 69128 | tf_op jit(solution)/shard_map/while/body/eval_jaxpr/ppermute | solution.py:26
  298.2 14.8 %collective-permute-start = (f32[3,1,15,128]{3,2,1,0:T(8,128)}, f32[3,1,15,128]{3,2,1,0:T(8,128)}, u32[]{:S(2)}, u32[]{:S(2)}) collective-permute-start(f32[3,1,15,128]{3,2,1,0:T(8,128)} %pad_maximum_fusion.22), channel_id=1, source_target_pairs={{0,16},{16,32},{32,48},{48,64},{64,80},{80,96},{96,112},{112,0},{1... | collective-permute-start | bytes 69128 | tf_op jit(solution)/shard_map/while/body/eval_jaxpr/ppermute | solution.py:26
  316.6 17.1 %copy-start.7 = (f32[12]{0:T(128)S(1)}, f32[12]{0:T(128)}, u32[]{:S(2)}) copy-start(f32[12]{0:T(128)} %get-tuple-element.660) | copy-start | bytes 148 | tf_op jit(solution)/shard_map/while
  316.6 40.1 %copy-start.1 = (f32[15,15,128]{2,1,0:T(8,128)S(1)}, f32[15,15,128]{2,1,0:T(8,128)}, u32[]{:S(2)}) copy-start(f32[15,15,128]{2,1,0:T(8,128)} %get-tuple-element.553) | copy-start | bytes 345604 | tf_op jit(solution)/shard_map/while
  316.6 40.1 %copy-start.2 = (f32[15,15,128]{2,1,0:T(8,128)S(1)}, f32[15,15,128]{2,1,0:T(8,128)}, u32[]{:S(2)}) copy-start(f32[15,15,128]{2,1,0:T(8,128)} %get-tuple-element.561) | copy-start | bytes 345604 | tf_op jit(solution)/shard_map/while
  316.6 40.1 %copy-start.3 = (f32[15,15,128]{2,1,0:T(8,128)S(1)}, f32[15,15,128]{2,1,0:T(8,128)}, u32[]{:S(2)}) copy-start(f32[15,15,128]{2,1,0:T(8,128)} %get-tuple-element.556) | copy-start | bytes 345604 | tf_op jit(solution)/shard_map/while
  360.7 3.3 collective-permute-start.3
  361.1 2.9 collective-permute-start.2
  421.0 14.8 %collective-permute-start.1 = (f32[3,1,15,128]{3,2,1,0:T(8,128)}, f32[3,1,15,128]{3,2,1,0:T(8,128)}, u32[]{:S(2)}, u32[]{:S(2)}) collective-permute-start(f32[3,1,15,128]{3,2,1,0:T(8,128)} %pad_maximum_fusion.23), channel_id=1, source_target_pairs={{0,112},{16,0},{32,16},{48,32},{64,48},{80,64},{96,80},{112,96},{1... | collective-permute-start | bytes 69128 | tf_op jit(solution)/shard_map/while/body/eval_jaxpr/ppermute | solution.py:26
  421.9 14.8 %collective-permute-start = (f32[3,1,15,128]{3,2,1,0:T(8,128)}, f32[3,1,15,128]{3,2,1,0:T(8,128)}, u32[]{:S(2)}, u32[]{:S(2)}) collective-permute-start(f32[3,1,15,128]{3,2,1,0:T(8,128)} %pad_maximum_fusion.22), channel_id=1, source_target_pairs={{0,16},{16,32},{32,48},{48,64},{64,80},{80,96},{96,112},{112,0},{1... | collective-permute-start | bytes 69128 | tf_op jit(solution)/shard_map/while/body/eval_jaxpr/ppermute | solution.py:26
  440.3 40.1 %copy-start.1 = (f32[15,15,128]{2,1,0:T(8,128)S(1)}, f32[15,15,128]{2,1,0:T(8,128)}, u32[]{:S(2)}) copy-start(f32[15,15,128]{2,1,0:T(8,128)} %get-tuple-element.553) | copy-start | bytes 345604 | tf_op jit(solution)/shard_map/while
  440.3 40.1 %copy-start.2 = (f32[15,15,128]{2,1,0:T(8,128)S(1)}, f32[15,15,128]{2,1,0:T(8,128)}, u32[]{:S(2)}) copy-start(f32[15,15,128]{2,1,0:T(8,128)} %get-tuple-element.561) | copy-start | bytes 345604 | tf_op jit(solution)/shard_map/while
  440.3 40.1 %copy-start.3 = (f32[15,15,128]{2,1,0:T(8,128)S(1)}, f32[15,15,128]{2,1,0:T(8,128)}, u32[]{:S(2)}) copy-start(f32[15,15,128]{2,1,0:T(8,128)} %get-tuple-element.556) | copy-start | bytes 345604 | tf_op jit(solution)/shard_map/while
  484.4 3.3 collective-permute-start.3
  484.8 2.9 collective-permute-start.2
  545.1 14.8 %collective-permute-start.1 = (f32[3,1,15,128]{3,2,1,0:T(8,128)}, f32[3,1,15,128]{3,2,1,0:T(8,128)}, u32[]{:S(2)}, u32[]{:S(2)}) collective-permute-start(f32[3,1,15,128]{3,2,1,0:T(8,128)} %pad_maximum_fusion.23), channel_id=1, source_target_pairs={{0,112},{16,0},{32,16},{48,32},{64,48},{80,64},{96,80},{112,96},{1... | collective-permute-start | bytes 69128 | tf_op jit(solution)/shard_map/while/body/eval_jaxpr/ppermute | solution.py:26
  546.0 14.8 %collective-permute-start = (f32[3,1,15,128]{3,2,1,0:T(8,128)}, f32[3,1,15,128]{3,2,1,0:T(8,128)}, u32[]{:S(2)}, u32[]{:S(2)}) collective-permute-start(f32[3,1,15,128]{3,2,1,0:T(8,128)} %pad_maximum_fusion.22), channel_id=1, source_target_pairs={{0,16},{16,32},{32,48},{48,64},{64,80},{80,96},{96,112},{112,0},{1... | collective-permute-start | bytes 69128 | tf_op jit(solution)/shard_map/while/body/eval_jaxpr/ppermute | solution.py:26
  564.4 17.1 %copy-start.7 = (f32[12]{0:T(128)S(1)}, f32[12]{0:T(128)}, u32[]{:S(2)}) copy-start(f32[12]{0:T(128)} %get-tuple-element.660) | copy-start | bytes 148 | tf_op jit(solution)/shard_map/while
  564.4 40.1 %copy-start.1 = (f32[15,15,128]{2,1,0:T(8,128)S(1)}, f32[15,15,128]{2,1,0:T(8,128)}, u32[]{:S(2)}) copy-start(f32[15,15,128]{2,1,0:T(8,128)} %get-tuple-element.553) | copy-start | bytes 345604 | tf_op jit(solution)/shard_map/while
  564.4 40.1 %copy-start.2 = (f32[15,15,128]{2,1,0:T(8,128)S(1)}, f32[15,15,128]{2,1,0:T(8,128)}, u32[]{:S(2)}) copy-start(f32[15,15,128]{2,1,0:T(8,128)} %get-tuple-element.561) | copy-start | bytes 345604 | tf_op jit(solution)/shard_map/while
  564.4 40.1 %copy-start.3 = (f32[15,15,128]{2,1,0:T(8,128)S(1)}, f32[15,15,128]{2,1,0:T(8,128)}, u32[]{:S(2)}) copy-start(f32[15,15,128]{2,1,0:T(8,128)} %get-tuple-element.556) | copy-start | bytes 345604 | tf_op jit(solution)/shard_map/while
  608.5 3.3 collective-permute-start.3
  609.0 2.9 collective-permute-start.2
  668.8 14.8 %collective-permute-start.1 = (f32[3,1,15,128]{3,2,1,0:T(8,128)}, f32[3,1,15,128]{3,2,1,0:T(8,128)}, u32[]{:S(2)}, u32[]{:S(2)}) collective-permute-start(f32[3,1,15,128]{3,2,1,0:T(8,128)} %pad_maximum_fusion.23), channel_id=1, source_target_pairs={{0,112},{16,0},{32,16},{48,32},{64,48},{80,64},{96,80},{112,96},{1... | collective-permute-start | bytes 69128 | tf_op jit(solution)/shard_map/while/body/eval_jaxpr/ppermute | solution.py:26
  669.8 14.8 %collective-permute-start = (f32[3,1,15,128]{3,2,1,0:T(8,128)}, f32[3,1,15,128]{3,2,1,0:T(8,128)}, u32[]{:S(2)}, u32[]{:S(2)}) collective-permute-start(f32[3,1,15,128]{3,2,1,0:T(8,128)} %pad_maximum_fusion.22), channel_id=1, source_target_pairs={{0,16},{16,32},{32,48},{48,64},{64,80},{80,96},{96,112},{112,0},{1... | collective-permute-start | bytes 69128 | tf_op jit(solution)/shard_map/while/body/eval_jaxpr/ppermute | solution.py:26
  688.2 40.1 %copy-start.1 = (f32[15,15,128]{2,1,0:T(8,128)S(1)}, f32[15,15,128]{2,1,0:T(8,128)}, u32[]{:S(2)}) copy-start(f32[15,15,128]{2,1,0:T(8,128)} %get-tuple-element.553) | copy-start | bytes 345604 | tf_op jit(solution)/shard_map/while
  688.2 40.1 %copy-start.2 = (f32[15,15,128]{2,1,0:T(8,128)S(1)}, f32[15,15,128]{2,1,0:T(8,128)}, u32[]{:S(2)}) copy-start(f32[15,15,128]{2,1,0:T(8,128)} %get-tuple-element.561) | copy-start | bytes 345604 | tf_op jit(solution)/shard_map/while
  688.2 40.1 %copy-start.3 = (f32[15,15,128]{2,1,0:T(8,128)S(1)}, f32[15,15,128]{2,1,0:T(8,128)}, u32[]{:S(2)}) copy-start(f32[15,15,128]{2,1,0:T(8,128)} %get-tuple-element.556) | copy-start | bytes 345604 | tf_op jit(solution)/shard_map/while
  732.2 3.3 collective-permute-start.3
  732.7 2.9 collective-permute-start.2
  (38 other events, 164.5 us)
where the time goes:
time: 790 us; the launch traced here: 786 us
  blocking collectives  474 us (60%)
  other arithmetic  171 us (22%)
  loops' own time  65 us (8%)
  starting transfers between devices  34.5 us (4%)
  local copies, waits for them, and re-layouts  33.5 us (4%)
  waiting for transfers between devices  8.47 us (1%)
    psum x65, blocking collectives, over_axes(): array = lax.psum(array, axis)  474 us
    another operation x1, loops' own time, per_device(): lax.fori_loop(0, ROUNDS, one_round, (speed_vectors, bin_population, start...  65 us
    ppermute x24, starting transfers between devices, from_behind(): return lax.ppermute(value, axis, pairs)  34.5 us
    reduce_sum x12, other arithmetic, collide_step(): jnp.sum(thermal * thermal)  26.1 us
    add x12, other arithmetic, rotate(): cosine_term * thermal[member]  25.3 us
    reduce_sum x12, other arithmetic, collide_step(): moment = jnp.sum(ensemble_snapshot * occupied[None], axis=1)  18.5 us
  transfers between devices with their start and end apart: 24, of which 6 were waited for; matrix products, arithmetic and copies ran while one was open for 8% of the time, Pallas kernels for 0%

commit v1 on v0

--- a/solution.py
+++ b/solution.py
@@ -16,7 +16,8 @@
 
 def over_axes(array, axes):
     for axis in axes:
-        array = lax.psum(array, axis)
+        shards = lax.all_gather(array, axis, axis=0, tiled=False)
+        array = shards.sum(axis=0)
     return array
 
 

time: 790 us -> 939 us (1.19)
  local copies, waits for them, and re-layouts: 33.5 us -> 163 us
  other arithmetic: 171 us -> 226 us
  blocking collectives: 474 us -> 435 us
    psum x65 -> x0, blocking collectives: 474 us -> none  [over_axes(): array = lax.psum(array, axis)]
    while x0 -> x60, blocking collectives: none -> 403 us
    while x120 -> x378, local copies, waits for them, and re-layouts: 0.29 us -> 116 us
    reduce_sum x0 -> x65, other arithmetic: none -> 41.9 us  [over_axes(): array = shards.sum(axis=0)]
    unnamed x0 -> x5, blocking collectives: none -> 31.8 us
    unnamed x6 -> x31, local copies, waits for them, and re-layouts: 4.07 us -> 13.8 us
  transfers between devices with their start and end apart: 24 -> 24, of which waited for: 6 -> 6; matrix products, arithmetic and copies ran while one was open for 8% -> 11% of each run, Pallas kernels for 0% -> 0%
where the time goes in v1:
time: 939 us; the launch traced here: 934 us
  blocking collectives  435 us (46%)
  other arithmetic  226 us (24%)
  local copies, waits for them, and re-layouts  163 us (17%)
  loops' own time  67.8 us (7%)
  starting transfers between devices  34.5 us (4%)
    while x60, blocking collectives  403 us
    while x378, local copies, waits for them, and re-layouts  116 us
    another operation x1, loops' own time, per_device(): lax.fori_loop(0, ROUNDS, one_round, (speed_vectors, bin_population, start...  67.8 us
    reduce_sum x65, other arithmetic, over_axes(): array = shards.sum(axis=0)  41.9 us
    ppermute x24, starting transfers between devices, from_behind(): return lax.ppermute(value, axis, pairs)  34.5 us
    unnamed x5, blocking collectives  31.8 us
    reduce_sum x12, other arithmetic, collide_step(): jnp.sum(thermal * thermal)  26.4 us
    add x12, other arithmetic, rotate(): cosine_term * thermal[member]  25.3 us
  transfers between devices with their start and end apart: 24, of which 6 were waited for; matrix products, arithmetic and copies ran while one was open for 11% of the time, Pallas kernels for 0%

profile of v1, /device:TPU:47, one launch (start us, length us, event | category | flops | bytes accessed | tf_op | source)
XLA Modules:
  0.0 933.9 jit_solution(9526465459926051743)
XLA Ops:
  6.8 6.7 all-reduce.10
  16.1 5.3 all-reduce.11
  30.3 7.0 all-reduce.13
  40.0 9.1 all-reduce.14
  49.7 884.2 %while.18 = (s32[]{:T(128)}, f32[3,6,15,15,128]{4,3,2,1,0:T(8,128)}, s32[15,15,128]{2,1,0:T(8,128)S(1)}, f32[12]{0:T(128)}, f32[]{:T(128)}, /*index=5*/s32[12]{0...) while((s32[]{:T(128)}, ...), condition=%wide.region_23.26_spmd, body=%wide.region_6.25_spmd.sunk | while | flops 29883344 | bytes 69058264 | solution.py:162
  88.3 8.2 all-reduce.25
  115.0 8.5 all-reduce.28
  126.4 9.4 %all-reduce.29 = f32[2]{0:T(128)S(1)} all-reduce(f32[2]{0:T(128)S(1)} %dynamic-update-slice.29), channel_id=1, replica_groups=mesh['bx_0'=4,'bx_1'=2,'by_0'=2,'by_1'=4,'by_2'=2] {'by_2'}, use_global_device_ids=true, to_apply=%add.4 | all-reduce | flops 2 | bytes 16 | tf_op jit(solution)/shard_map/while
  149.6 6.6 all-reduce.30
  158.2 5.3 all-reduce.31
  172.4 6.8 all-reduce.33
  181.3 11.8 %all-reduce.34 = f32[2]{0:T(128)S(1)} all-reduce(f32[2]{0:T(128)S(1)} %dynamic-update-slice.34), channel_id=1, replica_groups=mesh['bx_0'=4,'bx_1'=2,'by_0'=2,'by_1'=4,'by_2'=2] {'by_2'}, use_global_device_ids=true, to_apply=%add.9 | all-reduce | flops 2 | bytes 16 | tf_op jit(solution)/shard_map/while
  238.0 6.7 all-reduce.25
  263.3 5.7 all-reduce.28
  271.9 9.4 %all-reduce.29 = f32[2]{0:T(128)S(1)} all-reduce(f32[2]{0:T(128)S(1)} %dynamic-update-slice.29), channel_id=1, replica_groups=mesh['bx_0'=4,'bx_1'=2,'by_0'=2,'by_1'=4,'by_2'=2] {'by_2'}, use_global_device_ids=true, to_apply=%add.4 | all-reduce | flops 2 | bytes 16 | tf_op jit(solution)/shard_map/while
  295.0 7.8 all-reduce.30
  304.9 5.3 all-reduce.31
  319.0 7.7 all-reduce.33
  328.8 11.4 %all-reduce.34 = f32[2]{0:T(128)S(1)} all-reduce(f32[2]{0:T(128)S(1)} %dynamic-update-slice.34), channel_id=1, replica_groups=mesh['bx_0'=4,'bx_1'=2,'by_0'=2,'by_1'=4,'by_2'=2] {'by_2'}, use_global_device_ids=true, to_apply=%add.9 | all-reduce | flops 2 | bytes 16 | tf_op jit(solution)/shard_map/while
  385.1 6.0 all-reduce.25
  409.7 5.7 all-reduce.28
  418.2 9.0 all-reduce.29
  441.0 8.9 all-reduce.30
  451.9 5.3 all-reduce.31
  466.1 7.7 all-reduce.33
  475.9 11.0 %all-reduce.34 = f32[2]{0:T(128)S(1)} all-reduce(f32[2]{0:T(128)S(1)} %dynamic-update-slice.34), channel_id=1, replica_groups=mesh['bx_0'=4,'bx_1'=2,'by_0'=2,'by_1'=4,'by_2'=2] {'by_2'}, use_global_device_ids=true, to_apply=%add.9 | all-reduce | flops 2 | bytes 16 | tf_op jit(solution)/shard_map/while
  531.7 6.0 all-reduce.25
  541.1 5.3 all-reduce.26
  556.3 5.7 all-reduce.28
  564.9 9.0 all-reduce.29
  587.7 8.9 all-reduce.30
  598.6 5.3 all-reduce.31
  612.8 7.7 all-reduce.33
  622.5 11.4 %all-reduce.34 = f32[2]{0:T(128)S(1)} all-reduce(f32[2]{0:T(128)S(1)} %dynamic-update-slice.34), channel_id=1, replica_groups=mesh['bx_0'=4,'bx_1'=2,'by_0'=2,'by_1'=4,'by_2'=2] {'by_2'}, use_global_device_ids=true, to_apply=%add.9 | all-reduce | flops 2 | bytes 16 | tf_op jit(solution)/shard_map/while
  678.8 6.0 all-reduce.25
  703.4 5.7 all-reduce.28
  711.9 9.0 all-reduce.29
  734.8 8.9 all-reduce.30
  745.6 5.3 all-reduce.31
  759.8 7.7 all-reduce.33
  769.6 11.0 %all-reduce.34 = f32[2]{0:T(128)S(1)} all-reduce(f32[2]{0:T(128)S(1)} %dynamic-update-slice.34), channel_id=1, replica_groups=mesh['bx_0'=4,'bx_1'=2,'by_0'=2,'by_1'=4,'by_2'=2] {'by_2'}, use_global_device_ids=true, to_apply=%add.9 | all-reduce | flops 2 | bytes 16 | tf_op jit(solution)/shard_map/while
  825.4 6.0 all-reduce.25
  850.0 5.7 all-reduce.28
  858.6 9.0 all-reduce.29
  881.4 8.9 all-reduce.30
  892.3 5.3 all-reduce.31
  906.5 7.7 all-reduce.33
  916.3 11.4 %all-reduce.34 = f32[2]{0:T(128)S(1)} all-reduce(f32[2]{0:T(128)S(1)} %dynamic-update-slice.34), channel_id=1, replica_groups=mesh['bx_0'=4,'bx_1'=2,'by_0'=2,'by_1'=4,'by_2'=2] {'by_2'}, use_global_device_ids=true, to_apply=%add.9 | all-reduce | flops 2 | bytes 16 | tf_op jit(solution)/shard_map/while
  (829 shorter events, 506.5 us)
Async XLA Ops:
  0.9 13.2 %copy-start.18 = (u32[128]{0:T(128)S(1)}, u32[128]{0:T(128)}, u32[]{:S(2)}) copy-start(u32[128]{0:T(128)} %constant.414) | copy-start | bytes 1540
  0.9 21.1 %copy-start.20 = (u32[128]{0:T(128)S(1)}, u32[128]{0:T(128)}, u32[]{:S(2)}) copy-start(u32[128]{0:T(128)} %constant.419) | copy-start | bytes 1540
  0.9 27.5 %copy-start.22 = (u32[128]{0:T(128)S(1)}, u32[128]{0:T(128)}, u32[]{:S(2)}) copy-start(u32[128]{0:T(128)} %constant.424) | copy-start | bytes 1540
  0.9 37.1 %copy-start.24 = (u32[128]{0:T(128)S(1)}, u32[128]{0:T(128)}, u32[]{:S(2)}) copy-start(u32[128]{0:T(128)} %constant.429) | copy-start | bytes 1540
  0.9 48.8 %copy-start.11 = (s32[12]{0:T(128)S(1)}, s32[12]{0:T(128)}, u32[]{:S(2)}) copy-start(s32[12]{0:T(128)} %param.17) | copy-start | bytes 148
  0.9 48.8 %copy-start.13 = (s32[12]{0:T(128)S(1)}, s32[12]{0:T(128)}, u32[]{:S(2)}) copy-start(s32[12]{0:T(128)} %param.18) | copy-start | bytes 148
  56.3 21.8 %collective-permute-start.1 = (f32[3,1,15,128]{3,2,1,0:T(8,128)}, f32[3,1,15,128]{3,2,1,0:T(8,128)}, u32[]{:S(2)}, u32[]{:S(2)}) collective-permute-start(f32[3,1,15,128]{3,2,1,0:T(8,128)} %pad_maximum_fusion.23), channel_id=1, source_target_pairs={{0,112},{16,0},{32,16},{48,32},{64,48},{80,64},{96,80},{112,96},{1... | collective-permute-start | bytes 69128 | tf_op jit(solution)/shard_map/while/body/eval_jaxpr/ppermute | solution.py:27
  58.1 20.8 %collective-permute-start = (f32[3,1,15,128]{3,2,1,0:T(8,128)}, f32[3,1,15,128]{3,2,1,0:T(8,128)}, u32[]{:S(2)}, u32[]{:S(2)}) collective-permute-start(f32[3,1,15,128]{3,2,1,0:T(8,128)} %pad_maximum_fusion.22), channel_id=1, source_target_pairs={{0,16},{16,32},{32,48},{48,64},{64,80},{80,96},{96,112},{112,0},{1... | collective-permute-start | bytes 69128 | tf_op jit(solution)/shard_map/while/body/eval_jaxpr/ppermute | solution.py:27
  82.5 54.8 %copy-start.1 = (f32[15,15,128]{2,1,0:T(8,128)S(1)}, f32[15,15,128]{2,1,0:T(8,128)}, u32[]{:S(2)}) copy-start(f32[15,15,128]{2,1,0:T(8,128)} %get-tuple-element.553) | copy-start | bytes 345604 | tf_op jit(solution)/shard_map/while
  82.5 54.8 %copy-start.2 = (f32[15,15,128]{2,1,0:T(8,128)S(1)}, f32[15,15,128]{2,1,0:T(8,128)}, u32[]{:S(2)}) copy-start(f32[15,15,128]{2,1,0:T(8,128)} %get-tuple-element.561) | copy-start | bytes 345604 | tf_op jit(solution)/shard_map/while
  82.5 54.8 %copy-start.3 = (f32[15,15,128]{2,1,0:T(8,128)S(1)}, f32[15,15,128]{2,1,0:T(8,128)}, u32[]{:S(2)}) copy-start(f32[15,15,128]{2,1,0:T(8,128)} %get-tuple-element.556) | copy-start | bytes 345604 | tf_op jit(solution)/shard_map/while
  141.3 3.4 collective-permute-start.3
  141.7 2.9 collective-permute-start.2
  206.0 21.8 %collective-permute-start.1 = (f32[3,1,15,128]{3,2,1,0:T(8,128)}, f32[3,1,15,128]{3,2,1,0:T(8,128)}, u32[]{:S(2)}, u32[]{:S(2)}) collective-permute-start(f32[3,1,15,128]{3,2,1,0:T(8,128)} %pad_maximum_fusion.23), channel_id=1, source_target_pairs={{0,112},{16,0},{32,16},{48,32},{64,48},{80,64},{96,80},{112,96},{1... | collective-permute-start | bytes 69128 | tf_op jit(solution)/shard_map/while/body/eval_jaxpr/ppermute | solution.py:27
  207.0 21.6 %collective-permute-start = (f32[3,1,15,128]{3,2,1,0:T(8,128)}, f32[3,1,15,128]{3,2,1,0:T(8,128)}, u32[]{:S(2)}, u32[]{:S(2)}) collective-permute-start(f32[3,1,15,128]{3,2,1,0:T(8,128)} %pad_maximum_fusion.22), channel_id=1, source_target_pairs={{0,16},{16,32},{32,48},{48,64},{64,80},{80,96},{96,112},{112,0},{1... | collective-permute-start | bytes 69128 | tf_op jit(solution)/shard_map/while/body/eval_jaxpr/ppermute | solution.py:27
  232.2 50.5 %copy-start.1 = (f32[15,15,128]{2,1,0:T(8,128)S(1)}, f32[15,15,128]{2,1,0:T(8,128)}, u32[]{:S(2)}) copy-start(f32[15,15,128]{2,1,0:T(8,128)} %get-tuple-element.553) | copy-start | bytes 345604 | tf_op jit(solution)/shard_map/while
  232.2 50.5 %copy-start.2 = (f32[15,15,128]{2,1,0:T(8,128)S(1)}, f32[15,15,128]{2,1,0:T(8,128)}, u32[]{:S(2)}) copy-start(f32[15,15,128]{2,1,0:T(8,128)} %get-tuple-element.561) | copy-start | bytes 345604 | tf_op jit(solution)/shard_map/while
  232.2 50.5 %copy-start.3 = (f32[15,15,128]{2,1,0:T(8,128)S(1)}, f32[15,15,128]{2,1,0:T(8,128)}, u32[]{:S(2)}) copy-start(f32[15,15,128]{2,1,0:T(8,128)} %get-tuple-element.556) | copy-start | bytes 345604 | tf_op jit(solution)/shard_map/while
  286.7 3.3 collective-permute-start.3
  287.2 2.9 collective-permute-start.2
  353.1 21.8 %collective-permute-start.1 = (f32[3,1,15,128]{3,2,1,0:T(8,128)}, f32[3,1,15,128]{3,2,1,0:T(8,128)}, u32[]{:S(2)}, u32[]{:S(2)}) collective-permute-start(f32[3,1,15,128]{3,2,1,0:T(8,128)} %pad_maximum_fusion.23), channel_id=1, source_target_pairs={{0,112},{16,0},{32,16},{48,32},{64,48},{80,64},{96,80},{112,96},{1... | collective-permute-start | bytes 69128 | tf_op jit(solution)/shard_map/while/body/eval_jaxpr/ppermute | solution.py:27
  354.0 21.6 %collective-permute-start = (f32[3,1,15,128]{3,2,1,0:T(8,128)}, f32[3,1,15,128]{3,2,1,0:T(8,128)}, u32[]{:S(2)}, u32[]{:S(2)}) collective-permute-start(f32[3,1,15,128]{3,2,1,0:T(8,128)} %pad_maximum_fusion.22), channel_id=1, source_target_pairs={{0,16},{16,32},{32,48},{48,64},{64,80},{80,96},{96,112},{112,0},{1... | collective-permute-start | bytes 69128 | tf_op jit(solution)/shard_map/while/body/eval_jaxpr/ppermute | solution.py:27
  379.2 49.5 %copy-start.1 = (f32[15,15,128]{2,1,0:T(8,128)S(1)}, f32[15,15,128]{2,1,0:T(8,128)}, u32[]{:S(2)}) copy-start(f32[15,15,128]{2,1,0:T(8,128)} %get-tuple-element.553) | copy-start | bytes 345604 | tf_op jit(solution)/shard_map/while
  379.2 49.5 %copy-start.2 = (f32[15,15,128]{2,1,0:T(8,128)S(1)}, f32[15,15,128]{2,1,0:T(8,128)}, u32[]{:S(2)}) copy-start(f32[15,15,128]{2,1,0:T(8,128)} %get-tuple-element.561) | copy-start | bytes 345604 | tf_op jit(solution)/shard_map/while
  379.2 49.5 %copy-start.3 = (f32[15,15,128]{2,1,0:T(8,128)S(1)}, f32[15,15,128]{2,1,0:T(8,128)}, u32[]{:S(2)}) copy-start(f32[15,15,128]{2,1,0:T(8,128)} %get-tuple-element.556) | copy-start | bytes 345604 | tf_op jit(solution)/shard_map/while
  432.7 3.3 collective-permute-start.3
  433.2 2.9 collective-permute-start.2
  499.8 21.8 %collective-permute-start.1 = (f32[3,1,15,128]{3,2,1,0:T(8,128)}, f32[3,1,15,128]{3,2,1,0:T(8,128)}, u32[]{:S(2)}, u32[]{:S(2)}) collective-permute-start(f32[3,1,15,128]{3,2,1,0:T(8,128)} %pad_maximum_fusion.23), channel_id=1, source_target_pairs={{0,112},{16,0},{32,16},{48,32},{64,48},{80,64},{96,80},{112,96},{1... | collective-permute-start | bytes 69128 | tf_op jit(solution)/shard_map/while/body/eval_jaxpr/ppermute | solution.py:27
  500.7 21.6 %collective-permute-start = (f32[3,1,15,128]{3,2,1,0:T(8,128)}, f32[3,1,15,128]{3,2,1,0:T(8,128)}, u32[]{:S(2)}, u32[]{:S(2)}) collective-permute-start(f32[3,1,15,128]{3,2,1,0:T(8,128)} %pad_maximum_fusion.22), channel_id=1, source_target_pairs={{0,16},{16,32},{32,48},{48,64},{64,80},{80,96},{96,112},{112,0},{1... | collective-permute-start | bytes 69128 | tf_op jit(solution)/shard_map/while/body/eval_jaxpr/ppermute | solution.py:27
  525.9 49.5 %copy-start.1 = (f32[15,15,128]{2,1,0:T(8,128)S(1)}, f32[15,15,128]{2,1,0:T(8,128)}, u32[]{:S(2)}) copy-start(f32[15,15,128]{2,1,0:T(8,128)} %get-tuple-element.553) | copy-start | bytes 345604 | tf_op jit(solution)/shard_map/while
  525.9 49.5 %copy-start.2 = (f32[15,15,128]{2,1,0:T(8,128)S(1)}, f32[15,15,128]{2,1,0:T(8,128)}, u32[]{:S(2)}) copy-start(f32[15,15,128]{2,1,0:T(8,128)} %get-tuple-element.561) | copy-start | bytes 345604 | tf_op jit(solution)/shard_map/while
  525.9 49.5 %copy-start.3 = (f32[15,15,128]{2,1,0:T(8,128)S(1)}, f32[15,15,128]{2,1,0:T(8,128)}, u32[]{:S(2)}) copy-start(f32[15,15,128]{2,1,0:T(8,128)} %get-tuple-element.556) | copy-start | bytes 345604 | tf_op jit(solution)/shard_map/while
  579.4 3.3 collective-permute-start.3
  579.8 2.9 collective-permute-start.2
  646.8 21.8 %collective-permute-start.1 = (f32[3,1,15,128]{3,2,1,0:T(8,128)}, f32[3,1,15,128]{3,2,1,0:T(8,128)}, u32[]{:S(2)}, u32[]{:S(2)}) collective-permute-start(f32[3,1,15,128]{3,2,1,0:T(8,128)} %pad_maximum_fusion.23), channel_id=1, source_target_pairs={{0,112},{16,0},{32,16},{48,32},{64,48},{80,64},{96,80},{112,96},{1... | collective-permute-start | bytes 69128 | tf_op jit(solution)/shard_map/while/body/eval_jaxpr/ppermute | solution.py:27
  647.7 21.6 %collective-permute-start = (f32[3,1,15,128]{3,2,1,0:T(8,128)}, f32[3,1,15,128]{3,2,1,0:T(8,128)}, u32[]{:S(2)}, u32[]{:S(2)}) collective-permute-start(f32[3,1,15,128]{3,2,1,0:T(8,128)} %pad_maximum_fusion.22), channel_id=1, source_target_pairs={{0,16},{16,32},{32,48},{48,64},{64,80},{80,96},{96,112},{112,0},{1... | collective-permute-start | bytes 69128 | tf_op jit(solution)/shard_map/while/body/eval_jaxpr/ppermute | solution.py:27
  673.0 49.5 %copy-start.1 = (f32[15,15,128]{2,1,0:T(8,128)S(1)}, f32[15,15,128]{2,1,0:T(8,128)}, u32[]{:S(2)}) copy-start(f32[15,15,128]{2,1,0:T(8,128)} %get-tuple-element.553) | copy-start | bytes 345604 | tf_op jit(solution)/shard_map/while
  673.0 49.5 %copy-start.2 = (f32[15,15,128]{2,1,0:T(8,128)S(1)}, f32[15,15,128]{2,1,0:T(8,128)}, u32[]{:S(2)}) copy-start(f32[15,15,128]{2,1,0:T(8,128)} %get-tuple-element.561) | copy-start | bytes 345604 | tf_op jit(solution)/shard_map/while
  673.0 49.5 %copy-start.3 = (f32[15,15,128]{2,1,0:T(8,128)S(1)}, f32[15,15,128]{2,1,0:T(8,128)}, u32[]{:S(2)}) copy-start(f32[15,15,128]{2,1,0:T(8,128)} %get-tuple-element.556) | copy-start | bytes 345604 | tf_op jit(solution)/shard_map/while
  726.5 3.3 collective-permute-start.3
  726.9 2.9 collective-permute-start.2
  793.5 21.8 %collective-permute-start.1 = (f32[3,1,15,128]{3,2,1,0:T(8,128)}, f32[3,1,15,128]{3,2,1,0:T(8,128)}, u32[]{:S(2)}, u32[]{:S(2)}) collective-permute-start(f32[3,1,15,128]{3,2,1,0:T(8,128)} %pad_maximum_fusion.23), channel_id=1, source_target_pairs={{0,112},{16,0},{32,16},{48,32},{64,48},{80,64},{96,80},{112,96},{1... | collective-permute-start | bytes 69128 | tf_op jit(solution)/shard_map/while/body/eval_jaxpr/ppermute | solution.py:27
  794.4 21.6 %collective-permute-start = (f32[3,1,15,128]{3,2,1,0:T(8,128)}, f32[3,1,15,128]{3,2,1,0:T(8,128)}, u32[]{:S(2)}, u32[]{:S(2)}) collective-permute-start(f32[3,1,15,128]{3,2,1,0:T(8,128)} %pad_maximum_fusion.22), channel_id=1, source_target_pairs={{0,16},{16,32},{32,48},{48,64},{64,80},{80,96},{96,112},{112,0},{1... | collective-permute-start | bytes 69128 | tf_op jit(solution)/shard_map/while/body/eval_jaxpr/ppermute | solution.py:27
  819.6 49.5 %copy-start.1 = (f32[15,15,128]{2,1,0:T(8,128)S(1)}, f32[15,15,128]{2,1,0:T(8,128)}, u32[]{:S(2)}) copy-start(f32[15,15,128]{2,1,0:T(8,128)} %get-tuple-element.553) | copy-start | bytes 345604 | tf_op jit(solution)/shard_map/while
  819.6 49.5 %copy-start.2 = (f32[15,15,128]{2,1,0:T(8,128)S(1)}, f32[15,15,128]{2,1,0:T(8,128)}, u32[]{:S(2)}) copy-start(f32[15,15,128]{2,1,0:T(8,128)} %get-tuple-element.561) | copy-start | bytes 345604 | tf_op jit(solution)/shard_map/while
  819.6 49.5 %copy-start.3 = (f32[15,15,128]{2,1,0:T(8,128)S(1)}, f32[15,15,128]{2,1,0:T(8,128)}, u32[]{:S(2)}) copy-start(f32[15,15,128]{2,1,0:T(8,128)} %get-tuple-element.556) | copy-start | bytes 345604 | tf_op jit(solution)/shard_map/while
  873.1 3.3 collective-permute-start.3
  873.6 2.9 collective-permute-start.2
  (97 other events, 422.6 us)
